TPU v7x, 32 devices: a whole 2x2x4 slice. The times are simulated.
32 devices in a mesh: rep: 2 (over y), span: 2 (over core), seq: 4 (over z), tp: 2 (over x).
Axes of the slice: x: 2, y: 2, z: 4, core: 2. Of those that a mesh axis runs over, the one named last changes fastest.
Arguments:
- queries: bfloat16 [8, 512, 24, 128], P(('rep', 'span'), 'seq', 'tp'), parts along dimension 0, may hold values from -110 to 110
- key_states: bfloat16 [8, 512, 4, 128], P(('rep', 'span'), 'seq', 'tp'), parts along dimension 0, may hold values from -11 to 11
- value_states: bfloat16 [8, 512, 4, 128], P(('rep', 'span'), 'seq', 'tp'), parts along dimension 0, may hold values from -6 to 6
- out_weight: bfloat16 [3072, 6144], P('tp', 'seq'), may hold values from -0.109375 to 0.109375
- noise_table: float32 [64, 6144], P(None, 'tp'), may hold values from 0.5 to 2
- plan: int32 [8], P('rep'), parts along dimension 0, may hold values from 0 to 63
Outputs:
- branch_out: bfloat16 [8, 512, 6144], P(('rep', 'span'), 'seq', 'tp'), parts along dimension 0
There are 2 independent parts, one for each index of `rep`. A program takes and returns all parts, laid end to end along the dimension named above; an argument that names none is the same for every part. Nothing has to cross between parts.
All inputs are finite; a program needn't handle non-finite values.
Results may differ from a plain program's by a relative error of at most 0.014.
Values may be sent and summed in bfloat16 or wider, within the bound.
A program may use at most 128 MiB of HBM per device.

v0:
```python
import jax
import jax.numpy as jnp
from jax import lax
from jax.sharding import PartitionSpec as P


def fold_block(carried, query_rows, key_rows, value_rows, factor):
    maxima, totals, weighted = carried
    scores = (
        jnp.einsum("tkgd,skd->tkgs", query_rows, key_rows, preferred_element_type=jnp.float32)
        * factor
    )
    highest = jnp.maximum(maxima, jnp.max(scores, axis=-1))
    shrink = jnp.exp(maxima - highest)
    weights = jnp.exp(scores - highest[..., None])
    totals = totals * shrink + jnp.sum(weights, axis=-1)
    weighted = weighted * shrink[..., None] + jnp.einsum(
        "tkgs,skd->tkgd",
        weights.astype(jnp.bfloat16),
        value_rows,
        preferred_element_type=jnp.float32,
    )
    return (maxima * 0.0 + highest, totals, weighted)


def per_device(queries, key_states, value_states, out_weight, noise_table, plan):
    ch_dev, tok_dev, heads_local, head_size = queries.shape
    kv_local = key_states.shape[2]
    per_kv = heads_local // kv_local
    span_count = ch_dev * lax.axis_size("span")
    first_span = lax.axis_index("span") * ch_dev
    factor = head_size ** (-0.5)
    grouped = queries.reshape(ch_dev, tok_dev, kv_local, per_kv, head_size)
    start_max = jnp.full((ch_dev, tok_dev, kv_local, per_kv), -1e30, jnp.float32)
    start_tot = jnp.zeros((ch_dev, tok_dev, kv_local, per_kv), jnp.float32)
    start_acc = jnp.zeros((ch_dev, tok_dev, kv_local, per_kv, head_size), jnp.float32)
    span_rows = (
        lax.all_gather(key_states, "seq", axis=1, tiled=True),
        lax.all_gather(value_states, "seq", axis=1, tiled=True),
    )
    key_piece = lax.all_gather(span_rows[0], "span", axis=0, tiled=True)
    value_piece = lax.all_gather(span_rows[1], "span", axis=0, tiled=True)
    new_max = []
    new_tot = []
    new_acc = []
    for q_span in range(ch_dev):
        inner_state = (start_max[q_span], start_tot[q_span], start_acc[q_span])
        for k_span in range(span_count):

            def update(inner, q_span=q_span, k_span=k_span):
                return fold_block(
                    inner, grouped[q_span], key_piece[k_span], value_piece[k_span], factor
                )

            inner_state = lax.cond(
                k_span <= first_span + q_span, update, lambda inner: inner, inner_state
            )
        new_max.append(inner_state[0])
        new_tot.append(inner_state[1])
        new_acc.append(inner_state[2])
    attn = (
        (jnp.stack(new_acc) / jnp.stack(new_tot)[..., None])
        .reshape(ch_dev, tok_dev, heads_local * head_size)
        .astype(jnp.bfloat16)
    )
    columns = jnp.einsum(
        "ctf,fo->cto",
        lax.all_gather(attn, "seq", axis=1, tiled=True),
        out_weight,
        preferred_element_type=jnp.float32,
    )
    partial_out = lax.all_to_all(
        columns.astype(jnp.bfloat16), "seq", split_axis=1, concat_axis=2, tiled=True
    ).astype(columns.dtype)
    summed = lax.psum_scatter(
        partial_out.astype(jnp.bfloat16), "tp", scatter_dimension=2, tiled=True
    ).astype(jnp.float32)
    levels = lax.dynamic_slice_in_dim(plan, first_span, ch_dev)
    picks = (levels[:, None] == jnp.arange(noise_table.shape[0], dtype=jnp.int32)[None, :]).astype(
        jnp.float32
    )
    gates = jnp.dot(picks, noise_table, precision=lax.Precision.HIGHEST)
    return (summed * gates[:, None, :]).astype(jnp.bfloat16)


def solution(mesh):
    placed = (
        P(("rep", "span"), "seq", "tp", None),
        P(("rep", "span"), "seq", "tp", None),
        P(("rep", "span"), "seq", "tp", None),
        P("tp", "seq"),
        P(None, "tp"),
        P("rep"),
    )
    return jax.shard_map(
        per_device,
        mesh=mesh,
        in_specs=placed,
        out_specs=P(("rep", "span"), "seq", "tp"),
        check_vma=False,
    )
```

profile of v0, /device:TPU:0, one launch (start us, length us, event | category | flops | bytes accessed | tf_op | source)
XLA Modules:
  0.0 320.5 jit_solution(18199733619609409647)
XLA Ops:
  6.5 0.0 copy-start
  6.5 0.0 all-gather.4.cloned.1.call-start
  6.5 1.0 copy.63
  7.5 18.0 %all_gather.15 = bf16[2,512,2,128]{3,1,2,0:T(8,128)(2,1)} all-gather(bf16[2,128,2,128]{3,1,2,0:T(8,128)(2,1)S(1)} %copy.63), channel_id=1, replica_groups=mesh['rep'=2,'span'=2,'seq'=4,'tp'=2] {'seq'}, dimensions={1}, use_global_device_ids=true | all-gather | bytes 655360 | tf_op jit(solution)/shard_map/all_gather | solution.py:38
  25.5 0.0 all-gather.4.cloned.1.call-update
  25.6 0.0 all-gather.6.cloned.1.call-start
  25.6 0.9 copy.64
  26.5 17.0 %all_gather.17 = bf16[2,512,2,128]{3,1,2,0:T(8,128)(2,1)} all-gather(bf16[2,128,2,128]{3,1,2,0:T(8,128)(2,1)S(1)} %copy.64), channel_id=1, replica_groups=mesh['rep'=2,'span'=2,'seq'=4,'tp'=2] {'seq'}, dimensions={1}, use_global_device_ids=true | all-gather | bytes 655360 | tf_op jit(solution)/shard_map/all_gather | solution.py:39
  43.6 0.0 all-gather.6.cloned.1.call-update
  43.6 0.0 all-gather.8.cloned.1.call-start
  43.7 0.0 all-gather.4.cloned.1.call-done
  43.7 9.6 %all-gather.6.cloned.1.call-done = bf16[4,512,2,128]{3,1,2,0:T(8,128)(2,1)} async-done(((bf16[2,512,2,128]{3,1,2,0:T(8,128)(2,1)}), bf16[4,512,2,128]{3,1,2,0:T(8,128)(2,1)}) %all-gather.6.cloned.1.call-update) | async-done | bytes 1048592 | tf_op jit(solution)/shard_map/all_gather | solution.py:42
  53.3 6.1 %conditional.12 = (f32[128,2,6]{0,2,1:T(8,128)}, f32[128,2,6]{0,2,1:T(8,128)S(1)}, f32[128,2,6,128]{3,0,2,1:T(8,128)S(1)}) conditional(s32[]{:T(128)} %convert_element_type.70, () %tuple.93, (bf16[4,512,2,128]{3,1,2,0:T(8,128)(2,1)}, bf16[2,128,2,6,128]{4,1,3,2,0:T(8,128)(2,1)}, bf16[4,512,2,128]{3,1,2,0:T(8,128)(2,1)}) %tuple.190), branch_computations={%region_16.0_spmd, %region_17.0_spmd} | conditional | flops 409147392 | bytes 11210776 | solution.py:55
  53.3 1.7 bitcast_reduce_fusion.4
  55.0 0.6 exponential_multiply_fusion.1
  55.6 1.2 fusion.85
  56.8 0.7 fusion.104
  57.5 1.9 fusion.93
  59.4 6.2 %conditional.13 = ((f32[128,2,6]{0,2,1:T(8,128)}, f32[128,2,6]{0,2,1:T(8,128)S(1)}, f32[128,2,6,128]{3,0,2,1:T(8,128)S(1)})) conditional(s32[]{:T(128)} %convert_element_type.69, (f32[128,2,6]{0,2,1:T(8,128)}, f32[128,2,6]{0,2,1:T(8,128)S(1)}, f32[128,2,6,128]{3,0,2,1:T(8,128)S(1)}) %conditional.12, (f32[128,2,6]{0,2,1:T(8,128)}, ...), branch_computations={%region_20.0_spmd, %region_21.0_spmd} | conditional | flops 409344000 | bytes 12032032 | solution.py:55
  59.4 1.7 bitcast_reduce_fusion.5
  61.1 0.7 multiply_add_fusion.5
  61.8 0.5 fusion.107
  62.3 0.7 multiply_add_fusion.4
  63.0 0.6 copy.113
  63.6 2.0 fusion.115
  65.6 6.1 %conditional.8 = (f32[128,2,6]{0,2,1:T(8,128)}, f32[128,2,6]{0,2,1:T(8,128)S(1)}, f32[128,2,6,128]{3,0,2,1:T(8,128)S(1)}) conditional(s32[]{:T(128)} %convert_element_type.66, () %tuple.87, (bf16[4,512,2,128]{3,1,2,0:T(8,128)(2,1)}, bf16[2,128,2,6,128]{4,1,3,2,0:T(8,128)(2,1)}, bf16[4,512,2,128]{3,1,2,0:T(8,128)(2,1)}) %tuple.193), branch_computations={%region_0.0_spmd, %region_1.0_spmd} | conditional | flops 409147392 | bytes 11210776 | solution.py:55
  65.6 1.7 bitcast_reduce_fusion
  67.3 0.6 exponential_multiply_fusion
  67.9 1.2 fusion.2
  69.1 0.7 fusion.21
  69.8 1.9 fusion.10
  71.8 0.2 conditional.10
  72.0 1.5 conditional.15
  72.0 0.3 copy.68
  72.2 1.2 copy.102
  73.4 1.4 conditional.11
  73.4 0.3 copy.65
  73.7 1.2 copy.100
  74.9 0.1 div.11
  75.0 1.6 copy.73
  76.6 2.9 fusion.171
  79.5 0.0 all-gather.8.cloned.1.call-update
  79.6 0.0 reduce-scatter.2.cloned.1.call-start
  79.6 93.0 %all-gather.8.cloned.1.call-done = bf16[2,512,1536]{2,1,0:T(8,128)(2,1)} async-done(((bf16[2,128,1536]{2,1,0:T(8,128)(2,1)}), bf16[2,512,1536]{2,1,0:T(8,128)(2,1)}) %all-gather.8.cloned.1.call-update) | async-done | bytes 3145744 | tf_op jit(solution)/shard_map/all_gather | solution.py:68
  172.6 8.1 %fusion.168 = bf16[2,512,1536]{2,1,0:T(8,128)(2,1)S(1)} fusion(bf16[2,512,1536]{2,1,0:T(8,128)(2,1)} %all-gather.8.cloned.1.call-done, bf16[1536,1536]{1,0:T(8,128)(2,1)} %param.25), kind=kOutput, calls=%fused_computation.166 | convolution fusion | flops 4833411072 | bytes 11010048 | tf_op jit(solution)/shard_map/ctf,fo->cto/dot_general | solution.py:66
  180.7 3.2 %copy.74 = bf16[2,512,1536]{2,0,1:T(2,128)(2,1)S(1)} copy(bf16[2,512,1536]{2,1,0:T(8,128)(2,1)S(1)} %fusion.168) | data formatting | bytes 6291456 | tf_op jit(solution)/shard_map/convert_element_type | solution.py:73
  183.9 73.3 %all_to_all.18 = bf16[2,512,1536]{2,0,1:T(2,128)(2,1)S(1)} all-to-all(bf16[2,512,1536]{2,0,1:T(2,128)(2,1)S(1)} %copy.74), channel_id=1, replica_groups=mesh['rep'=2,'span'=2,'seq'=4,'tp'=2] {'seq'}, dimensions={1} | all-to-all | bytes 6291456 | tf_op jit(solution)/shard_map/all_to_all | solution.py:72
  257.2 4.1 %copy.75 = bf16[2,128,4,1536]{3,2,1,0:T(4,128)(2,1)} copy(bf16[2,128,4,1536]{3,0,1,2:T(2,128)(2,1)S(1)} %bitcast.326) | data formatting | bytes 6291456 | tf_op jit(solution)/shard_map/all_to_all | solution.py:72
  261.3 6.9 %all_to_all.16 = bf16[2,128,6144]{2,1,0:T(8,128)(2,1)} reshape(bf16[2,128,4,1536]{3,2,1,0:T(4,128)(2,1)} %copy.75) | data formatting | bytes 6291456 | tf_op jit(solution)/shard_map/all_to_all | solution.py:72
  268.3 0.0 copy-start.5
  268.3 0.0 reduce-scatter.2.cloned.1.call-update
  268.3 0.6 copy-done.5
  268.9 0.1 dynamic_slice.3
  269.0 0.0 copy-done
  269.0 0.4 fusion.172
  269.4 41.7 %reduce-scatter.2.cloned.1.call-done = bf16[2,128,3072]{2,1,0:T(8,128)(2,1)} async-done(((bf16[2,128,6144]{2,1,0:T(8,128)(2,1)}), bf16[2,128,3072]{2,1,0:T(8,128)(2,1)}) %reduce-scatter.2.cloned.1.call-update) | async-done | bytes 1572880 | tf_op jit(solution)/shard_map/reduce_scatter | solution.py:75
  311.1 2.9 multiply_convert_fusion
  (3 shorter events, 0.0 us)
Async XLA Ops:
  6.5 262.4 %copy-start = (f32[64,3072]{1,0:T(8,128)S(1)}, f32[64,3072]{1,0:T(8,128)}, u32[]{:S(2)}) copy-start(f32[64,3072]{1,0:T(8,128)} %param.26) | copy-start | bytes 2359300
  6.5 37.2 %all-gather.4.cloned.1.call-start = ((), (), s32[]{:S(2)}) async-start(), calls=%async_computation.2 | async-start | bytes 1572864 | tf_op jit(solution)/shard_map/all_gather | solution.py:41
  25.6 27.7 %all-gather.6.cloned.1.call-start = ((), (), s32[]{:S(2)}) async-start(), calls=%async_computation.3 | async-start | bytes 1572864 | tf_op jit(solution)/shard_map/all_gather | solution.py:42
  43.6 129.0 %all-gather.8.cloned.1.call-start = ((), (), s32[]{:S(2)}) async-start(), calls=%async_computation.4 | async-start | bytes 3932160 | tf_op jit(solution)/shard_map/all_gather | solution.py:68
  79.6 231.5 %reduce-scatter.2.cloned.1.call-start = ((), (), s32[]{:S(2)}) async-start(), calls=%async_computation.5 | async-start | bytes 4718592 | tf_op jit(solution)/shard_map/reduce_scatter | solution.py:75
  268.3 0.7 copy-start.5
Sparse Core Ops, SparseCore 0:
  25.7 10.8 all-gather.3
  43.7 9.5 all-gather.5
  79.7 92.8 all-gather.7
  268.4 42.6 reduce-scatter.1
where the time goes:
time: 322 us; the launch traced here: 321 us
  waiting for transfers between devices  144 us (45%)
  blocking collectives  108 us (34%)
  local copies, waits for them, and re-layouts  22.1 us (7%)
  matrix products  19.2 us (6%)
  between operations  13.2 us (4%)
  other arithmetic  12.9 us (4%)
    all_gather x1, waiting for transfers between devices, per_device(): lax.all_gather(attn, 'seq', axis=1, tiled=True)  93 us
    all_to_all x1, blocking collectives, per_device(): lax.all_to_all(columns.astype(jnp.bfloat16), 'seq', split_axis=1, concat_...  73.3 us
    reduce_scatter x1, waiting for transfers between devices, per_device(): lax.psum_scatter(partial_out.astype(jnp.bfloat16), 'tp', scatter_dimensio...  41.7 us
    all_gather x1, blocking collectives, per_device(): lax.all_gather(key_states, 'seq', axis=1, tiled=True)  18 us
    all_gather x1, blocking collectives, per_device(): lax.all_gather(value_states, 'seq', axis=1, tiled=True)  17 us
    all_to_all x2, local copies, waits for them, and re-layouts, per_device(): lax.all_to_all(columns.astype(jnp.bfloat16), 'seq', split_axis=1, concat_...  11 us
    all_gather x1, waiting for transfers between devices, per_device(): value_piece = lax.all_gather(span_rows[1], 'span', axis=0, tiled=True)  9.6 us
    dot_general x1, matrix products, per_device(): jnp.einsum('ctf,fo->cto', lax.all_gather(attn, 'seq', axis=1, tiled=True)...  8.06 us
  transfers between devices with their start and end apart: 4, of which 3 were waited for; matrix products, arithmetic and copies ran while one was open for 0% of the time, Pallas kernels for 0%

commit v1 on v0

--- a/solution.py
+++ b/solution.py
@@ -65,7 +65,7 @@
     )
     columns = jnp.einsum(
         "ctf,fo->cto",
-        lax.all_gather(attn, "seq", axis=1, tiled=True),
+        jnp.concatenate(lax.all_gather(attn, axis_name="seq"), axis=1),
         out_weight,
         preferred_element_type=jnp.float32,
     )

time: 322 us -> 320 us (level)
  no operation moved by 1% of the time
where the time goes in v1:
time: 320 us; the launch traced here: 319 us
  waiting for transfers between devices  143 us (45%)
  blocking collectives  108 us (34%)
  local copies, waits for them, and re-layouts  23.2 us (7%)
  matrix products  18.7 us (6%)
  between operations  13.2 us (4%)
  other arithmetic  11.7 us (4%)
    all_gather x1, waiting for transfers between devices, per_device(): lax.all_gather(attn, axis_name='seq')  92 us
    all_to_all x1, blocking collectives, per_device(): lax.all_to_all(columns.astype(jnp.bfloat16), 'seq', split_axis=1, concat_...  73.3 us
    reduce_scatter x1, waiting for transfers between devices, per_device(): lax.psum_scatter(partial_out.astype(jnp.bfloat16), 'tp', scatter_dimensio...  41.7 us
    all_gather x1, blocking collectives, per_device(): lax.all_gather(key_states, 'seq', axis=1, tiled=True)  18 us
    all_gather x1, blocking collectives, per_device(): lax.all_gather(value_states, 'seq', axis=1, tiled=True)  17 us
    all_to_all x2, local copies, waits for them, and re-layouts, per_device(): lax.all_to_all(columns.astype(jnp.bfloat16), 'seq', split_axis=1, concat_...  11 us
    all_gather x1, waiting for transfers between devices, per_device(): value_piece = lax.all_gather(span_rows[1], 'span', axis=0, tiled=True)  9.6 us
    dot_general x1, matrix products, per_device(): jnp.einsum('ctf,fo->cto', jnp.concatenate(lax.all_gather(attn, axis_name=...  7.58 us
  transfers between devices with their start and end apart: 4, of which 3 were waited for; matrix products, arithmetic and copies ran while one was open for 0% of the time, Pallas kernels for 0%

profile of v1, /device:TPU:0, one launch (start us, length us, event | category | flops | bytes accessed | tf_op | source)
XLA Modules:
  0.0 318.7 jit_solution(16168666967645279914)
XLA Ops:
  6.5 0.0 copy-start
  6.5 0.0 all-gather.4.cloned.1.call-start
  6.5 1.0 copy.59
  7.5 18.0 %all_gather.16 = bf16[2,512,2,128]{3,1,2,0:T(8,128)(2,1)} all-gather(bf16[2,128,2,128]{3,1,2,0:T(8,128)(2,1)S(1)} %copy.59), channel_id=1, replica_groups=mesh['rep'=2,'span'=2,'seq'=4,'tp'=2] {'seq'}, dimensions={1}, use_global_device_ids=true | all-gather | bytes 655360 | tf_op jit(solution)/shard_map/all_gather | solution.py:38
  25.5 0.0 all-gather.4.cloned.1.call-update
  25.6 0.0 all-gather.6.cloned.1.call-start
  25.6 0.9 copy.60
  26.5 17.0 %all_gather.18 = bf16[2,512,2,128]{3,1,2,0:T(8,128)(2,1)} all-gather(bf16[2,128,2,128]{3,1,2,0:T(8,128)(2,1)S(1)} %copy.60), channel_id=1, replica_groups=mesh['rep'=2,'span'=2,'seq'=4,'tp'=2] {'seq'}, dimensions={1}, use_global_device_ids=true | all-gather | bytes 655360 | tf_op jit(solution)/shard_map/all_gather | solution.py:39
  43.6 0.0 all-gather.6.cloned.1.call-update
  43.6 0.0 all-gather.8.cloned.1.call-start
  43.7 0.0 all-gather.4.cloned.1.call-done
  43.7 9.6 %all-gather.6.cloned.1.call-done = bf16[4,512,2,128]{3,1,2,0:T(8,128)(2,1)} async-done(((bf16[2,512,2,128]{3,1,2,0:T(8,128)(2,1)}), bf16[4,512,2,128]{3,1,2,0:T(8,128)(2,1)}) %all-gather.6.cloned.1.call-update) | async-done | bytes 1048592 | tf_op jit(solution)/shard_map/all_gather | solution.py:42
  53.3 6.1 %conditional.8 = (f32[128,2,6]{0,2,1:T(8,128)}, f32[128,2,6]{0,2,1:T(8,128)S(1)}, f32[128,2,6,128]{3,0,2,1:T(8,128)S(1)}) conditional(s32[]{:T(128)} %convert_element_type.73, () %tuple.87, (bf16[4,512,2,128]{3,1,2,0:T(8,128)(2,1)}, bf16[2,128,2,6,128]{4,1,3,2,0:T(8,128)(2,1)}, bf16[4,512,2,128]{3,1,2,0:T(8,128)(2,1)}) %tuple.180), branch_computations={%region_0.0_spmd, %region_1.0_spmd} | conditional | flops 409147392 | bytes 11210776 | solution.py:55
  53.3 1.7 bitcast_reduce_fusion
  55.0 0.6 exponential_multiply_fusion
  55.6 1.2 fusion.2
  56.8 0.7 fusion.21
  57.5 1.9 fusion.10
  59.4 6.1 %conditional.12 = (f32[128,2,6]{0,2,1:T(8,128)}, f32[128,2,6]{0,2,1:T(8,128)S(1)}, f32[128,2,6,128]{3,0,2,1:T(8,128)S(1)}) conditional(s32[]{:T(128)} %convert_element_type.77, () %tuple.93, (bf16[4,512,2,128]{3,1,2,0:T(8,128)(2,1)}, bf16[2,128,2,6,128]{4,1,3,2,0:T(8,128)(2,1)}, bf16[4,512,2,128]{3,1,2,0:T(8,128)(2,1)}) %tuple.183), branch_computations={%region_16.0_spmd, %region_17.0_spmd} | conditional | flops 409147392 | bytes 11210776 | solution.py:55
  59.4 1.7 bitcast_reduce_fusion.4
  61.1 0.6 exponential_multiply_fusion.1
  61.7 1.2 fusion.85
  62.9 0.7 fusion.104
  63.6 1.9 fusion.93
  65.5 6.2 %conditional.13 = ((f32[128,2,6]{0,2,1:T(8,128)}, f32[128,2,6]{0,2,1:T(8,128)S(1)}, f32[128,2,6,128]{3,0,2,1:T(8,128)S(1)})) conditional(s32[]{:T(128)} %convert_element_type.76, (f32[128,2,6]{0,2,1:T(8,128)}, f32[128,2,6]{0,2,1:T(8,128)S(1)}, f32[128,2,6,128]{3,0,2,1:T(8,128)S(1)}) %conditional.12, (f32[128,2,6]{0,2,1:T(8,128)}, ...), branch_computations={%region_20.0_spmd, %region_21.0_spmd} | conditional | flops 409344000 | bytes 12032032 | solution.py:55
  65.5 1.7 bitcast_reduce_fusion.5
  67.2 0.7 multiply_add_fusion.5
  67.9 0.5 fusion.107
  68.4 0.7 multiply_add_fusion.4
  69.1 2.0 fusion.115
  71.2 0.6 copy.104
  71.8 1.2 conditional.11
  71.8 1.2 copy.61
  72.9 1.2 conditional.15
  72.9 1.2 copy.64
  74.1 0.1 div.18
  74.2 1.8 fusion.171
  76.0 1.2 copy.67
  77.2 0.0 all-gather.8.cloned.1.call-update
  77.2 0.0 reduce-scatter.2.cloned.1.call-start
  77.2 92.0 %all-gather.8.cloned.1.call-done = bf16[4,2,128,1536]{3,2,1,0:T(8,128)(2,1)} async-done(((bf16[1,2,128,1536]{3,2,1,0:T(8,128)(2,1)}), bf16[4,2,128,1536]{3,2,1,0:T(8,128)(2,1)}) %all-gather.8.cloned.1.call-update) | async-done | bytes 3145744 | tf_op jit(solution)/shard_map/all_gather | solution.py:68
  169.2 2.1 copy.68
  171.3 7.6 %fusion.168 = bf16[2,512,1536]{2,1,0:T(8,128)(2,1)S(1)} fusion(bf16[2,512,1536]{2,1,0:T(8,128)(2,1)S(1)} %bitcast.331, bf16[1536,1536]{1,0:T(8,128)(2,1)} %param.25), kind=kOutput, calls=%fused_computation.166 | convolution fusion | flops 4833411072 | bytes 11010048 | tf_op jit(solution)/shard_map/ctf,fo->cto/dot_general | solution.py:66
  178.9 3.2 %copy.69 = bf16[2,512,1536]{2,0,1:T(2,128)(2,1)S(1)} copy(bf16[2,512,1536]{2,1,0:T(8,128)(2,1)S(1)} %fusion.168) | data formatting | bytes 6291456 | tf_op jit(solution)/shard_map/convert_element_type | solution.py:73
  182.1 73.3 %all_to_all.18 = bf16[2,512,1536]{2,0,1:T(2,128)(2,1)S(1)} all-to-all(bf16[2,512,1536]{2,0,1:T(2,128)(2,1)S(1)} %copy.69), channel_id=1, replica_groups=mesh['rep'=2,'span'=2,'seq'=4,'tp'=2] {'seq'}, dimensions={1} | all-to-all | bytes 6291456 | tf_op jit(solution)/shard_map/all_to_all | solution.py:72
  255.4 4.1 %copy.70 = bf16[2,128,4,1536]{3,2,1,0:T(4,128)(2,1)} copy(bf16[2,128,4,1536]{3,0,1,2:T(2,128)(2,1)S(1)} %bitcast.328) | data formatting | bytes 6291456 | tf_op jit(solution)/shard_map/all_to_all | solution.py:72
  259.5 6.9 %all_to_all.16 = bf16[2,128,6144]{2,1,0:T(8,128)(2,1)} reshape(bf16[2,128,4,1536]{3,2,1,0:T(4,128)(2,1)} %copy.70) | data formatting | bytes 6291456 | tf_op jit(solution)/shard_map/all_to_all | solution.py:72
  266.5 0.0 copy-start.5
  266.5 0.0 reduce-scatter.2.cloned.1.call-update
  266.5 0.6 copy-done.5
  267.1 0.1 dynamic_slice.3
  267.2 0.0 copy-done
  267.2 0.4 fusion.172
  267.6 41.7 %reduce-scatter.2.cloned.1.call-done = bf16[2,128,3072]{2,1,0:T(8,128)(2,1)} async-done(((bf16[2,128,6144]{2,1,0:T(8,128)(2,1)}), bf16[2,128,3072]{2,1,0:T(8,128)(2,1)}) %reduce-scatter.2.cloned.1.call-update) | async-done | bytes 1572880 | tf_op jit(solution)/shard_map/reduce_scatter | solution.py:75
  309.3 2.9 multiply_convert_fusion
  (4 shorter events, 0.0 us)
Async XLA Ops:
  6.5 260.7 %copy-start = (f32[64,3072]{1,0:T(8,128)S(1)}, f32[64,3072]{1,0:T(8,128)}, u32[]{:S(2)}) copy-start(f32[64,3072]{1,0:T(8,128)} %param.26) | copy-start | bytes 2359300
  6.5 37.2 %all-gather.4.cloned.1.call-start = ((), (), s32[]{:S(2)}) async-start(), calls=%async_computation.2 | async-start | bytes 1572864 | tf_op jit(solution)/shard_map/all_gather | solution.py:41
  25.6 27.7 %all-gather.6.cloned.1.call-start = ((), (), s32[]{:S(2)}) async-start(), calls=%async_computation.3 | async-start | bytes 1572864 | tf_op jit(solution)/shard_map/all_gather | solution.py:42
  43.6 125.6 %all-gather.8.cloned.1.call-start = ((), (), s32[]{:S(2)}) async-start(), calls=%async_computation.4 | async-start | bytes 3932160 | tf_op jit(solution)/shard_map/all_gather | solution.py:68
  77.2 232.1 %reduce-scatter.2.cloned.1.call-start = ((), (), s32[]{:S(2)}) async-start(), calls=%async_computation.5 | async-start | bytes 4718592 | tf_op jit(solution)/shard_map/reduce_scatter | solution.py:75
  266.5 0.7 copy-start.5
Sparse Core Ops, SparseCore 0:
  25.7 10.8 all-gather.3
  43.7 9.5 all-gather.5
  77.3 91.8 all-gather.7
  266.6 42.6 reduce-scatter.1
